TPU v7x, 1024 devices: a whole 4x8x16 slice. The times are simulated.
1024 devices in a mesh: gx: 8 (over y), gy: 8 (over x, core), gz: 16 (over z).
Axes of the slice: x: 4, y: 8, z: 16, core: 2. Of those that a mesh axis runs over, the one named last changes fastest.
Arguments:
- residual_in: float32 [8, 16, 128, 512], P('gx', 'gy', 'gz'), may hold values from -6 to 6
- geometry: float32 [3, 8, 16, 128], P(None, 'gx', 'gy', 'gz'), may hold values from 0.5 to 2
- eig_top: float32 [2], replicated, may hold values from 1.5 to 2.5
- coarse_rows: float32 [8, 24, 128, 11, 128], P('gx', 'gy', 'gz'), may hold values from -0.21875 to 0.21875
- block_ids: int32 [8, 8, 16, 11], P('gx', 'gy', 'gz'), may hold values from 0 to 2047, as said below
Outputs:
- correction: float32 [8, 16, 128, 512], P('gx', 'gy', 'gz')
Inputs may be any that keep to these rules, and one draw needn't show every extreme that they name: `block_ids`: the 11 ids of one row block are distinct.
All inputs are finite; a program needn't handle non-finite values.
Results may differ from a plain program's by a relative error of at most 0.00018.
Values sent between devices are 32-bit elements; how exact they have to be, the bound alone decides.
A program may use at most 64 MiB of HBM per device.

v0:
```python
import math

import jax
import jax.numpy as jnp
import numpy as np
from jax import lax
from jax.sharding import Mesh
from jax.sharding import PartitionSpec as P

NF = 8
NM = 4
NC = 2
GY = ("gy_0", "gy_1")


FULL_PRECISION = lax.Precision.HIGHEST


def with_halo(cells, sides, width):
    for axis, dim in sides:
        count = lax.axis_size(axis)
        head = lax.slice_in_dim(cells, 0, width, axis=dim)
        tail = lax.slice_in_dim(cells, cells.shape[dim] - width, cells.shape[dim], axis=dim)
        cells = jnp.concatenate(
            [
                lax.ppermute(tail, axis, [(i, (i + 1) % count) for i in range(count)]),
                cells,
                lax.ppermute(head, axis, [((i + 1) % count, i) for i in range(count)]),
            ],
            axis=dim,
        )
    return cells


def gathered_by_axis(array, axes, dim):
    if not axes:
        return array
    nearer = lax.all_gather(array, axes[-1], axis=dim, tiled=True)
    return gathered_by_axis(nearer, axes[:-1], dim)


def legendre_pair(point, degree):
    previous = 1.0
    current = point
    for order in range(1, degree):
        following = ((2 * order + 1) * point * current - order * previous) / (order + 1)
        previous = current
        current = following
    return (current, previous)


def gll_tables(points):
    degree = points - 1
    node_list = []
    for index in range(points):
        guess = -math.cos(math.pi * index / degree)
        for sweep in range(100):
            high_val, low_val = legendre_pair(guess, degree)
            guess = guess - (guess * high_val - low_val) / (points * high_val)
        node_list.append(guess)
    node_list[0] = -1.0
    node_list[degree] = 1.0
    node_pos = np.array(node_list)
    at_nodes = np.array([legendre_pair(value, degree)[0] for value in node_list])
    weights = 2.0 / (degree * (degree + 1) * at_nodes**2)
    derivative = np.zeros((points, points))
    for row_pos in range(points):
        for col_pos in range(points):
            if row_pos != col_pos:
                derivative[row_pos, col_pos] = at_nodes[row_pos] / (
                    at_nodes[col_pos] * (node_pos[row_pos] - node_pos[col_pos])
                )
    derivative[0, 0] = -degree * (degree + 1) / 4.0
    derivative[degree, degree] = degree * (degree + 1) / 4.0
    stiffness = derivative.T @ (weights[:, None] * derivative)
    return (node_pos, weights, stiffness)


def interp_table(fine_pts, coarse_pts):
    fine_nodes = gll_tables(fine_pts)[0]
    coarse_nodes = gll_tables(coarse_pts)[0]
    lagrange = np.ones((fine_pts, coarse_pts))
    for col_pos in range(coarse_pts):
        for other_pos in range(coarse_pts):
            if other_pos != col_pos:
                lagrange[:, col_pos] *= (fine_nodes - coarse_nodes[other_pos]) / (
                    coarse_nodes[col_pos] - coarse_nodes[other_pos]
                )
    return lagrange


def level_tables(points):
    node_pos, weights, stiffness = gll_tables(points)
    return (jnp.asarray(weights, jnp.float32), jnp.asarray(stiffness, jnp.float32))


def local_apply(nodal, coeffs, weights, stiffness):
    plane_w = weights[:, None] * weights[None, :]
    term_x = jnp.einsum("ia,...abc->...ibc", stiffness, nodal, precision=FULL_PRECISION) * plane_w
    term_y = (
        jnp.einsum("jb,...abc->...ajc", stiffness, nodal, precision=FULL_PRECISION)
        * plane_w[:, None, :]
    )
    term_z = (
        jnp.einsum("kc,...abc->...abk", stiffness, nodal, precision=FULL_PRECISION)
        * plane_w[:, :, None]
    )
    return (
        coeffs[0][..., None, None, None] * term_x
        + coeffs[1][..., None, None, None] * term_y
        + coeffs[2][..., None, None, None] * term_z
    )


def local_diagonal(coeffs, weights, stiffness):
    stiff_diag = jnp.diag(stiffness)
    part_x = stiff_diag[:, None, None] * weights[None, :, None] * weights[None, None, :]
    part_y = weights[:, None, None] * stiff_diag[None, :, None] * weights[None, None, :]
    part_z = weights[:, None, None] * weights[None, :, None] * stiff_diag[None, None, :]
    return (
        coeffs[0][..., None, None, None] * part_x
        + coeffs[1][..., None, None, None] * part_y
        + coeffs[2][..., None, None, None] * part_z
    )


def chebyshev(residual, initial, top_eig, operate, inverse_diag):
    center = 0.55 * top_eig
    spread_eig = 0.45 * top_eig
    sigma_ratio = center / spread_eig
    rho_first = 1.0 / sigma_ratio
    rho_next = 1.0 / (2.0 * sigma_ratio - rho_first)
    if initial is None:
        current = residual
    else:
        current = residual - operate(initial)
    step_one = inverse_diag * current / center
    iterate = step_one if initial is None else initial + step_one
    second_res = residual - operate(iterate)
    step_two = rho_first * rho_next * step_one + 2.0 * rho_next / spread_eig * (
        inverse_diag * second_res
    )
    return iterate + step_two


def prolong(nodal, lagrange):
    nodal = jnp.einsum("ia,...abc->...ibc", lagrange, nodal, precision=FULL_PRECISION)
    nodal = jnp.einsum("jb,...abc->...ajc", lagrange, nodal, precision=FULL_PRECISION)
    return jnp.einsum("kc,...abc->...abk", lagrange, nodal, precision=FULL_PRECISION)


def restrict(nodal, lagrange):
    nodal = jnp.einsum("ia,...ibc->...abc", lagrange, nodal, precision=FULL_PRECISION)
    nodal = jnp.einsum("jb,...ajc->...abc", lagrange, nodal, precision=FULL_PRECISION)
    return jnp.einsum("kc,...abk->...abc", lagrange, nodal, precision=FULL_PRECISION)


def multiplicity(points, elem_y, total_y):
    degree = points - 1
    first_node = (jnp.arange(points) == 0).astype(jnp.float32)
    last_node = (jnp.arange(points) == degree).astype(jnp.float32)
    side_x = 1.0 + first_node + last_node
    low_flag = (elem_y > 0).astype(jnp.float32)
    high_flag = (elem_y < total_y - 1).astype(jnp.float32)
    side_y = 1.0 + low_flag[:, None] * first_node[None, :] + high_flag[:, None] * last_node[None, :]
    return (
        side_x[None, None, None, :, None, None]
        * side_y[None, :, None, None, :, None]
        * side_x[None, None, None, None, None, :]
    )


def put_faces(nodal, new_left, new_right, point_axis):
    degree = nodal.shape[point_axis] - 1
    middle = lax.slice_in_dim(nodal, 1, degree, axis=point_axis)
    return jnp.concatenate(
        [jnp.expand_dims(new_left, point_axis), middle, jnp.expand_dims(new_right, point_axis)],
        axis=point_axis,
    )


def local_pass(nodal, direction):
    elem_axis = 1 + direction
    point_axis = 4 + direction
    degree = nodal.shape[point_axis] - 1
    extent = nodal.shape[elem_axis]
    left_face = jnp.take(nodal, 0, axis=point_axis)
    right_face = jnp.take(nodal, degree, axis=point_axis)
    summed = lax.slice_in_dim(right_face, 0, extent - 1, axis=elem_axis) + lax.slice_in_dim(
        left_face, 1, extent, axis=elem_axis
    )
    new_right = jnp.concatenate(
        [summed, lax.slice_in_dim(right_face, extent - 1, extent, axis=elem_axis)], axis=elem_axis
    )
    new_left = jnp.concatenate(
        [lax.slice_in_dim(left_face, 0, 1, axis=elem_axis), summed], axis=elem_axis
    )
    return put_faces(nodal, new_left, new_right, point_axis)


def fold_axis(point_grid, elem_axis):
    shape_g = point_grid.shape
    extent = shape_g[elem_axis]
    degree = shape_g[elem_axis + 1] - 1
    main_part = lax.slice_in_dim(point_grid, 0, degree, axis=elem_axis + 1).reshape(
        shape_g[:elem_axis] + (extent * degree,) + shape_g[elem_axis + 2 :]
    )
    last_elem = lax.index_in_dim(point_grid, extent - 1, elem_axis, keepdims=False)
    last_plane = lax.index_in_dim(last_elem, degree, elem_axis, keepdims=True)
    return jnp.concatenate([main_part, last_plane], axis=elem_axis)


def unfold_axis(point_grid, elem_axis, extent):
    shape_g = point_grid.shape
    degree = (shape_g[elem_axis] - 1) // extent
    main_part = lax.slice_in_dim(point_grid, 0, extent * degree, axis=elem_axis).reshape(
        shape_g[:elem_axis] + (extent, degree) + shape_g[elem_axis + 1 :]
    )
    tail_plane = lax.slice_in_dim(
        point_grid, degree, extent * degree + 1, stride=degree, axis=elem_axis
    )
    return jnp.concatenate(
        [main_part, jnp.expand_dims(tail_plane, elem_axis + 1)], axis=elem_axis + 1
    )


def shell_sum(nodal):
    for direction in (0, 1, 2):
        nodal = local_pass(nodal, direction)
    extents = nodal.shape[1:4]
    point_grid = jnp.transpose(nodal, (0, 1, 4, 2, 5, 3, 6))
    for elem_axis in (1, 2, 3):
        point_grid = fold_axis(point_grid, elem_axis)
    padded = with_halo(point_grid, (("gx", 1), (GY, 2), ("gz", 3)), 1)
    y_len = padded.shape[2]
    y_pos = jnp.arange(y_len)[None, None, :, None]
    at_wall = (y_pos == 0) & (lax.axis_index(GY) == 0) | (y_pos == y_len - 1) & (
        lax.axis_index(GY) == lax.axis_size(GY) - 1
    )
    padded = jnp.where(at_wall, 0.0, padded)
    for elem_axis in (1, 2, 3):
        length = padded.shape[elem_axis] - 2
        shape_list = [1, 1, 1, 1]
        shape_list[elem_axis] = length
        position = jnp.arange(length).reshape(shape_list)
        center_part = lax.slice_in_dim(padded, 1, length + 1, axis=elem_axis)
        lower_side = lax.slice_in_dim(padded, 0, length, axis=elem_axis)
        upper_side = lax.slice_in_dim(padded, 2, length + 2, axis=elem_axis)
        padded = (
            center_part
            + jnp.where(position == 0, lower_side, 0.0)
            + jnp.where(position == length - 1, upper_side, 0.0)
        )
    point_grid = unfold_axis(padded, 3, extents[2])
    point_grid = unfold_axis(point_grid, 2, extents[1])
    point_grid = unfold_axis(point_grid, 1, extents[0])
    return jnp.transpose(point_grid, (0, 1, 3, 5, 2, 4, 6))


def direct_sum(nodal):
    return shell_sum(nodal)


def coarse_solve(low_res, coarse_rows, block_ids):
    cx_count, cy_count, cz_count = low_res.shape[:3]
    flat_nodes = low_res.reshape(cx_count, cy_count, cz_count, -1)
    top_flag = (lax.axis_index(GY) == lax.axis_size(GY) - 1).astype(jnp.float32)
    owned_vals = jnp.concatenate(
        [flat_nodes[..., 0], flat_nodes[:, cy_count - 1 :, :, 2] * top_flag], axis=1
    )
    block_count = coarse_rows.shape[3]
    block_width = coarse_rows.shape[4]
    rows_flat = coarse_rows.reshape(-1, block_count * block_width)
    contrib = jnp.dot(owned_vals.reshape(-1), rows_flat, precision=FULL_PRECISION).reshape(
        block_count, block_width
    )
    my_ids = block_ids.reshape(-1)
    my_float = my_ids.astype(jnp.float32)
    matches = (
        my_float[:, None] == gathered_by_axis(my_float, ("gy_1", "gy_0", "gz", "gx"), 0)[None, :]
    ).astype(jnp.float32)
    picked = jnp.zeros_like(contrib) + jnp.dot(
        matches,
        gathered_by_axis(contrib, ("gy_1", "gy_0", "gz", "gx"), 0),
        precision=FULL_PRECISION,
    )
    solved = jnp.dot(rows_flat, picked.reshape(-1), precision=FULL_PRECISION).reshape(
        cx_count, cy_count + 1, cz_count
    )
    corner_zero = solved[:, :cy_count]
    top_values = solved[:, cy_count:] * top_flag
    corner_two = jnp.concatenate(
        [jnp.zeros((cx_count, cy_count - 1, cz_count), jnp.float32), top_values], axis=1
    )
    zero_nodes = jnp.zeros_like(corner_zero)
    spread_nodes = jnp.stack(
        [
            corner_zero,
            zero_nodes,
            corner_two,
            zero_nodes,
            zero_nodes,
            zero_nodes,
            zero_nodes,
            zero_nodes,
        ],
        axis=-1,
    )
    return direct_sum(spread_nodes.reshape(cx_count, cy_count, cz_count, 2, 2, 2)[None])[0]


def on_device(residual_in, geometry, eig_top, coarse_rows, block_ids):
    cx_count, cy_count, cz_count = residual_in.shape[:3]
    fine_w, fine_k = level_tables(NF)
    mid_w, mid_k = level_tables(NM)
    up_mid = jnp.asarray(interp_table(NF, NM), jnp.float32)
    up_low = jnp.asarray(interp_table(NM, NC), jnp.float32)
    elem_y = lax.axis_index(GY) * cy_count + jnp.arange(cy_count)
    total_y = lax.axis_size(GY) * cy_count
    source = residual_in.reshape(cx_count, cy_count, cz_count, NF, NF, NF)
    stacked = direct_sum(jnp.stack([source, local_diagonal(geometry, fine_w, fine_k)]))
    fine_res = stacked[0]
    fine_inv = 1.0 / stacked[1]

    def fine_op(nodal):
        return direct_sum(local_apply(nodal, geometry, fine_w, fine_k)[None])[0]

    def mid_op(nodal):
        return direct_sum(local_apply(nodal, geometry, mid_w, mid_k)[None])[0]

    fine_x = chebyshev(fine_res, None, eig_top[0], fine_op, fine_inv)
    fine_left = fine_res - fine_op(fine_x)
    mid_src = restrict(fine_left / multiplicity(NF, elem_y, total_y), up_mid)
    stacked = direct_sum(jnp.stack([mid_src, local_diagonal(geometry, mid_w, mid_k)]))
    mid_res = stacked[0]
    mid_inv = 1.0 / stacked[1]
    mid_x = chebyshev(mid_res, None, eig_top[1], mid_op, mid_inv)
    mid_left = mid_res - mid_op(mid_x)
    low_res = direct_sum(restrict(mid_left / multiplicity(NM, elem_y, total_y), up_low)[None])[0]
    low_u = coarse_solve(low_res, coarse_rows, block_ids)
    mid_x = chebyshev(mid_res, mid_x + prolong(low_u, up_low), eig_top[1], mid_op, mid_inv)
    fine_x = chebyshev(fine_res, fine_x + prolong(mid_x, up_mid), eig_top[0], fine_op, fine_inv)
    return fine_x.reshape(cx_count, cy_count, cz_count, NF**3)


def solution(mesh):
    split = Mesh(
        mesh.devices.reshape(mesh.shape["gx"], 4, 2, mesh.shape["gz"]), ("gx", "gy_0", "gy_1", "gz")
    )
    placed = (
        P("gx", GY, "gz", None),
        P(None, "gx", GY, "gz"),
        P(),
        P("gx", GY, "gz", None, None),
        P("gx", GY, "gz", None),
    )
    return jax.shard_map(
        on_device, mesh=split, in_specs=placed, out_specs=P("gx", GY, "gz", None), check_vma=False
    )
```

profile of v0, /device:TPU:1, one launch (start us, length us, event | category | flops | bytes accessed | tf_op | source)
XLA Modules:
  0.0 583.0 jit_solution(2090233881475483811)
XLA Ops:
  15.5 2.5 copy.1583
  20.2 2.5 copy.1584
  26.1 4.0 collective-permute-start
  30.1 3.8 collective-permute-start.1
  37.3 2.1 collective-permute-start.2
  39.4 11.3 %collective-permute-start.3 = (f32[2,10,1,57]{3,0,2,1:T(2,128)S(1)}, f32[2,10,1,57]{3,0,2,1:T(2,128)S(1)}, u32[]{:S(2)}, u32[]{:S(2)}) collective-permute-start(f32[2,10,1,57]{3,0,2,1:T(2,128)S(1)} %get-tuple-element.416), channel_id=1, source_target_pairs={{16,0},{32,16},{48,32},{64,48},{80,64},{96,80},{112,96},{0,112},{1... | collective-permute-start | bytes 13688 | tf_op jit(solution)/shard_map/ppermute | solution.py:28
  53.8 9.1 %collective-permute-start.5 = (f32[2,10,17,1]{3,0,2,1:T(2,128)S(1)}, f32[2,10,17,1]{3,0,2,1:T(2,128)S(1)}, u32[]{:S(2)}, u32[]{:S(2)}) collective-permute-start(f32[2,10,17,1]{3,0,2,1:T(2,128)S(1)} %get-tuple-element.414), channel_id=1, source_target_pairs={{1,0},{2,1},{3,2},{4,3},{5,4},{6,5},{7,6},{8,7},{9,8},{10,9},{11,1... | collective-permute-start | bytes 4088 | tf_op jit(solution)/shard_map/ppermute | solution.py:28
  80.1 2.2 collective-permute-start.6
  82.3 4.3 collective-permute-start.7
  90.5 2.6 collective-permute-done.9
  95.4 5.2 collective-permute-start.11
  112.3 4.8 collective-permute-start.12
  117.2 2.2 collective-permute-start.13
  119.7 2.4 collective-permute-done.13
  122.2 2.3 collective-permute-start.14
  129.8 5.5 collective-permute-start.17
  144.0 4.0 collective-permute-start.18
  148.0 2.5 collective-permute-start.19
  152.9 2.2 collective-permute-start.20
  155.2 2.3 collective-permute-start.21
  160.4 5.2 collective-permute-start.23
  170.9 3.8 collective-permute-start.24
  174.7 2.7 collective-permute-start.25
  179.1 2.3 collective-permute-start.26
  181.4 3.3 collective-permute-start.27
  187.7 5.2 collective-permute-start.29
  197.4 2.9 collective-permute-start.30
  200.3 3.6 collective-permute-start.31
  206.2 4.3 collective-permute-start.33
  211.5 2.2 collective-permute-start.34
  213.7 4.8 collective-permute-start.35
  222.5 2.8 collective-permute-start.36
  225.3 4.1 collective-permute-start.37
  230.2 5.4 collective-permute-start.39
  236.6 3.0 collective-permute-start.40
  239.6 4.0 collective-permute-start.41
  245.3 19.1 %all-gather.4 = f32[8,11,128]{2,1,0:T(8,128)S(1)} all-gather(f32[1,11,128]{2,1,0:T(8,128)S(1)} %copy.1864), channel_id=1, replica_groups=mesh['gx'=8,'gy_0'=4,'gy_1'=2,'gz'=16] {'gx'}, dimensions={0}, use_global_device_ids=true | all-gather | bytes 50688 | tf_op jit(solution)/shard_map/all_gather | solution.py:38
  264.4 28.4 %all_gather.29 = f32[1408,128]{1,0:T(8,128)} all-gather(f32[88,128]{1,0:T(8,128)S(1)} %reshape.3055), channel_id=1, replica_groups=mesh['gx'=8,'gy_0'=4,'gy_1'=2,'gz'=16] {'gz'}, dimensions={0}, use_global_device_ids=true | all-gather | bytes 765952 | tf_op jit(solution)/shard_map/all_gather | solution.py:38
  292.9 56.5 %all-gather.8.cloned.1.call-done = f32[5632,128]{1,0:T(8,128)} async-done(((f32[1408,128]{1,0:T(8,128)}), f32[5632,128]{1,0:T(8,128)}) %all-gather.8.cloned.1.call-update) | async-done | bytes 2883600 | tf_op jit(solution)/shard_map/all_gather | solution.py:38
  353.4 13.2 %all-reduce.1 = f32[88]{0:T(128)S(1)} all-reduce(f32[88]{0:T(128)S(1)} %fusion.355), channel_id=2, replica_groups=mesh['gx'=8,'gy_0'=4,'gy_1'=2,'gz'=16] {'gx'}, use_global_device_ids=true, to_apply=%add.1 | all-reduce | flops 88 | bytes 704
  366.9 26.2 %all-reduce.2 = f32[1408]{0:T(1024)S(1)} all-reduce(f32[1408]{0:T(1024)S(1)} %dynamic-update-slice.31), channel_id=3, replica_groups=mesh['gx'=8,'gy_0'=4,'gy_1'=2,'gz'=16] {'gz'}, use_global_device_ids=true, to_apply=%add.2 | all-reduce | flops 1408 | bytes 11264
  393.1 9.1 %all-gather.2 = f32[1,1,1,5632]{3,2,1,0:T(1,128)S(1)} all-gather(f32[1,1,1,1408]{3,2,1,0:T(1,128)S(1)} %reshape.3053), channel_id=4, replica_groups=mesh['gx'=8,'gy_0'=4,'gy_1'=2,'gz'=16] {'gy_0'}, dimensions={3}, use_global_device_ids=true | all-gather | bytes 28160 | tf_op jit(solution)/shard_map/all_gather | solution.py:38
  402.2 15.8 %all-gather.3 = f32[1,1,1,11264]{3,2,1,0:T(1,128)S(1)} all-gather(f32[1,1,1,5632]{3,2,1,0:T(1,128)S(1)} %all-gather.2), channel_id=5, replica_groups=mesh['gx'=8,'gy_0'=4,'gy_1'=2,'gz'=16] {'gy_1'}, dimensions={3}, use_global_device_ids=true | all-gather | bytes 67584 | tf_op jit(solution)/shard_map/all_gather | solution.py:38
  418.0 4.7 convolution_bitcast_fusion.18
  426.3 4.6 collective-permute-start.43
  437.6 4.6 collective-permute-start.47
  448.4 5.1 collective-permute-start.49
  461.6 5.1 collective-permute-start.53
  471.6 3.5 collective-permute-start.54
  475.1 3.5 collective-permute-start.55
  479.8 2.0 collective-permute-start.56
  481.9 3.1 collective-permute-start.57
  486.0 3.2 collective-permute-start.58
  489.2 4.1 collective-permute-start.59
  506.4 3.6 collective-permute-start.60
  510.0 2.9 collective-permute-start.61
  516.5 4.3 collective-permute-start.63
  522.0 3.6 collective-permute-start.64
  525.6 3.4 collective-permute-start.65
  548.0 3.1 collective-permute-start.66
  551.1 3.4 collective-permute-start.67
  557.0 5.2 collective-permute-start.69
  563.3 2.9 collective-permute-start.70
  566.2 3.6 collective-permute-start.71
  (791 shorter events, 175.7 us)
Async XLA Ops:
  6.5 342.8 %all-gather.8.cloned.1.call-start = ((), (), s32[]{:S(2)}) async-start(), calls=%async_computation | async-start | bytes 3604480 | tf_op jit(solution)/shard_map/all_gather | solution.py:38
  26.1 11.0 %collective-permute-start = (f32[2,1,15,57]{2,1,3,0:T(1,128)S(1)}, f32[2,1,15,57]{2,1,3,0:T(1,128)S(1)}, u32[]{:S(2)}, u32[]{:S(2)}) collective-permute-start(f32[2,1,15,57]{2,1,3,0:T(1,128)S(1)} %get-tuple-element.403), channel_id=1, source_target_pairs={{0,128},{128,256},{256,384},{384,512},{512,640},{640,768},{768,896... | collective-permute-start | bytes 20528 | tf_op jit(solution)/shard_map/ppermute | solution.py:26
  30.1 7.1 %collective-permute-start.1 = (f32[2,1,15,57]{2,1,3,0:T(1,128)S(1)}, f32[2,1,15,57]{2,1,3,0:T(1,128)S(1)}, u32[]{:S(2)}, u32[]{:S(2)}) collective-permute-start(f32[2,1,15,57]{2,1,3,0:T(1,128)S(1)} %get-tuple-element.404), channel_id=1, source_target_pairs={{128,0},{256,128},{384,256},{512,384},{640,512},{768,640},{896,768... | collective-permute-start | bytes 20528 | tf_op jit(solution)/shard_map/ppermute | solution.py:28
  37.3 14.0 %collective-permute-start.2 = (f32[2,10,1,57]{3,0,2,1:T(2,128)S(1)}, f32[2,10,1,57]{3,0,2,1:T(2,128)S(1)}, u32[]{:S(2)}, u32[]{:S(2)}) collective-permute-start(f32[2,10,1,57]{3,0,2,1:T(2,128)S(1)} %get-tuple-element.415), channel_id=1, source_target_pairs={{0,16},{16,32},{32,48},{48,64},{64,80},{80,96},{96,112},{112,0},{1... | collective-permute-start | bytes 13688 | tf_op jit(solution)/shard_map/ppermute | solution.py:26
  39.4 12.1 %collective-permute-start.3 = (f32[2,10,1,57]{3,0,2,1:T(2,128)S(1)}, f32[2,10,1,57]{3,0,2,1:T(2,128)S(1)}, u32[]{:S(2)}, u32[]{:S(2)}) collective-permute-start(f32[2,10,1,57]{3,0,2,1:T(2,128)S(1)} %get-tuple-element.416), channel_id=1, source_target_pairs={{16,0},{32,16},{48,32},{64,48},{80,64},{96,80},{112,96},{0,112},{1... | collective-permute-start | bytes 13688 | tf_op jit(solution)/shard_map/ppermute | solution.py:28
  51.8 13.5 %collective-permute-start.4 = (f32[2,10,17,1]{3,0,2,1:T(2,128)S(1)}, f32[2,10,17,1]{3,0,2,1:T(2,128)S(1)}, u32[]{:S(2)}, u32[]{:S(2)}) collective-permute-start(f32[2,10,17,1]{3,0,2,1:T(2,128)S(1)} %get-tuple-element.413), channel_id=1, source_target_pairs={{0,1},{1,2},{2,3},{3,4},{4,5},{5,6},{6,7},{7,8},{8,9},{9,10},{10,1... | collective-permute-start | bytes 4088 | tf_op jit(solution)/shard_map/ppermute | solution.py:26
  53.8 12.5 %collective-permute-start.5 = (f32[2,10,17,1]{3,0,2,1:T(2,128)S(1)}, f32[2,10,17,1]{3,0,2,1:T(2,128)S(1)}, u32[]{:S(2)}, u32[]{:S(2)}) collective-permute-start(f32[2,10,17,1]{3,0,2,1:T(2,128)S(1)} %get-tuple-element.414), channel_id=1, source_target_pairs={{1,0},{2,1},{3,2},{4,3},{5,4},{6,5},{7,6},{8,7},{9,8},{10,9},{11,1... | collective-permute-start | bytes 4088 | tf_op jit(solution)/shard_map/ppermute | solution.py:28
  80.1 6.7 %collective-permute-start.6 = (f32[1,1,15,57]{2,1,3,0:T(1,128)S(1)}, f32[1,1,15,57]{2,1,3,0:T(1,128)S(1)}, u32[]{:S(2)}, u32[]{:S(2)}) collective-permute-start(f32[1,1,15,57]{2,1,3,0:T(1,128)S(1)} %get-tuple-element.411), channel_id=1, source_target_pairs={{0,128},{128,256},{256,384},{384,512},{512,640},{640,768},{768,896... | collective-permute-start | bytes 10268 | tf_op jit(solution)/shard_map/ppermute | solution.py:26
  82.3 5.4 collective-permute-start.7
  93.5 7.8 %collective-permute-start.10 = (f32[1,10,17,1]{3,0,2,1:T(1,128)S(1)}, f32[1,10,17,1]{3,0,2,1:T(1,128)S(1)}, u32[]{:S(2)}, u32[]{:S(2)}) collective-permute-start(f32[1,10,17,1]{3,0,2,1:T(1,128)S(1)} %get-tuple-element.434), channel_id=1, source_target_pairs={{0,1},{1,2},{2,3},{3,4},{4,5},{5,6},{6,7},{7,8},{8,9},{9,10},{10,1... | collective-permute-start | bytes 2048 | tf_op jit(solution)/shard_map/ppermute | solution.py:26
  95.4 6.5 %collective-permute-start.11 = (f32[1,10,17,1]{3,0,2,1:T(1,128)S(1)}, f32[1,10,17,1]{3,0,2,1:T(1,128)S(1)}, u32[]{:S(2)}, u32[]{:S(2)}) collective-permute-start(f32[1,10,17,1]{3,0,2,1:T(1,128)S(1)} %get-tuple-element.435), channel_id=1, source_target_pairs={{1,0},{2,1},{3,2},{4,3},{5,4},{6,5},{7,6},{8,7},{9,8},{10,9},{11,1... | collective-permute-start | bytes 2048 | tf_op jit(solution)/shard_map/ppermute | solution.py:28
  112.3 7.3 %collective-permute-start.12 = (f32[1,1,15,57]{2,1,3,0:T(1,128)S(1)}, f32[1,1,15,57]{2,1,3,0:T(1,128)S(1)}, u32[]{:S(2)}, u32[]{:S(2)}) collective-permute-start(f32[1,1,15,57]{2,1,3,0:T(1,128)S(1)} %get-tuple-element.409), channel_id=1, source_target_pairs={{0,128},{128,256},{256,384},{384,512},{512,640},{640,768},{768,896... | collective-permute-start | bytes 10268 | tf_op jit(solution)/shard_map/ppermute | solution.py:26
  117.2 4.9 collective-permute-start.13
  127.9 7.4 %collective-permute-start.16 = (f32[1,10,17,1]{3,0,2,1:T(1,128)S(1)}, f32[1,10,17,1]{3,0,2,1:T(1,128)S(1)}, u32[]{:S(2)}, u32[]{:S(2)}) collective-permute-start(f32[1,10,17,1]{3,0,2,1:T(1,128)S(1)} %get-tuple-element.432), channel_id=1, source_target_pairs={{0,1},{1,2},{2,3},{3,4},{4,5},{5,6},{6,7},{7,8},{8,9},{9,10},{10,1... | collective-permute-start | bytes 2048 | tf_op jit(solution)/shard_map/ppermute | solution.py:26
  129.8 6.6 %collective-permute-start.17 = (f32[1,10,17,1]{3,0,2,1:T(1,128)S(1)}, f32[1,10,17,1]{3,0,2,1:T(1,128)S(1)}, u32[]{:S(2)}, u32[]{:S(2)}) collective-permute-start(f32[1,10,17,1]{3,0,2,1:T(1,128)S(1)} %get-tuple-element.433), channel_id=1, source_target_pairs={{1,0},{2,1},{3,2},{4,3},{5,4},{6,5},{7,6},{8,7},{9,8},{10,9},{11,1... | collective-permute-start | bytes 2048 | tf_op jit(solution)/shard_map/ppermute | solution.py:28
  144.0 6.7 %collective-permute-start.18 = (f32[2,1,7,25]{2,1,3,0:T(1,128)S(1)}, f32[2,1,7,25]{2,1,3,0:T(1,128)S(1)}, u32[]{:S(2)}, u32[]{:S(2)}) collective-permute-start(f32[2,1,7,25]{2,1,3,0:T(1,128)S(1)} %get-tuple-element.426), channel_id=1, source_target_pairs={{0,128},{128,256},{256,384},{384,512},{512,640},{640,768},{768,896... | collective-permute-start | bytes 4208 | tf_op jit(solution)/shard_map/ppermute | solution.py:26
  148.0 4.8 collective-permute-start.19
  152.9 5.2 collective-permute-start.20
  158.5 7.7 %collective-permute-start.22 = (f32[2,6,9,1]{3,0,2,1:T(2,128)S(1)}, f32[2,6,9,1]{3,0,2,1:T(2,128)S(1)}, u32[]{:S(2)}, u32[]{:S(2)}) collective-permute-start(f32[2,6,9,1]{3,0,2,1:T(2,128)S(1)} %get-tuple-element.498), channel_id=1, source_target_pairs={{0,1},{1,2},{2,3},{3,4},{4,5},{5,6},{6,7},{7,8},{8,9},{9,10},{10,1... | collective-permute-start | bytes 1304 | tf_op jit(solution)/shard_map/ppermute | solution.py:26
  160.4 6.4 %collective-permute-start.23 = (f32[2,6,9,1]{3,0,2,1:T(2,128)S(1)}, f32[2,6,9,1]{3,0,2,1:T(2,128)S(1)}, u32[]{:S(2)}, u32[]{:S(2)}) collective-permute-start(f32[2,6,9,1]{3,0,2,1:T(2,128)S(1)} %get-tuple-element.499), channel_id=1, source_target_pairs={{1,0},{2,1},{3,2},{4,3},{5,4},{6,5},{7,6},{8,7},{9,8},{10,9},{11,1... | collective-permute-start | bytes 1304 | tf_op jit(solution)/shard_map/ppermute | solution.py:28
  170.9 6.6 %collective-permute-start.24 = (f32[1,1,7,25]{3,0,2,1:T(1,128)S(1)}, f32[1,1,7,25]{3,0,2,1:T(1,128)S(1)}, u32[]{:S(2)}, u32[]{:S(2)}) collective-permute-start(f32[1,1,7,25]{3,0,2,1:T(1,128)S(1)} %get-tuple-element.529), channel_id=1, source_target_pairs={{0,128},{128,256},{256,384},{384,512},{512,640},{640,768},{768,896... | collective-permute-start | bytes 2108 | tf_op jit(solution)/shard_map/ppermute | solution.py:26
  174.7 4.3 collective-permute-start.25
  179.1 6.4 %collective-permute-start.26 = (f32[1,6,1,25]{3,0,2,1:T(1,128)S(1)}, f32[1,6,1,25]{3,0,2,1:T(1,128)S(1)}, u32[]{:S(2)}, u32[]{:S(2)}) collective-permute-start(f32[1,6,1,25]{3,0,2,1:T(1,128)S(1)} %get-tuple-element.508), channel_id=1, source_target_pairs={{0,16},{16,32},{32,48},{48,64},{64,80},{80,96},{96,112},{112,0},{1... | collective-permute-start | bytes 1808 | tf_op jit(solution)/shard_map/ppermute | solution.py:26
  185.7 7.2 %collective-permute-start.28 = (f32[1,6,9,1]{3,0,2,1:T(1,128)S(1)}, f32[1,6,9,1]{3,0,2,1:T(1,128)S(1)}, u32[]{:S(2)}, u32[]{:S(2)}) collective-permute-start(f32[1,6,9,1]{3,0,2,1:T(1,128)S(1)} %get-tuple-element.537), channel_id=1, source_target_pairs={{0,1},{1,2},{2,3},{3,4},{4,5},{5,6},{6,7},{7,8},{8,9},{9,10},{10,1... | collective-permute-start | bytes 656 | tf_op jit(solution)/shard_map/ppermute | solution.py:26
  187.7 6.1 %collective-permute-start.29 = (f32[1,6,9,1]{3,0,2,1:T(1,128)S(1)}, f32[1,6,9,1]{3,0,2,1:T(1,128)S(1)}, u32[]{:S(2)}, u32[]{:S(2)}) collective-permute-start(f32[1,6,9,1]{3,0,2,1:T(1,128)S(1)} %get-tuple-element.538), channel_id=1, source_target_pairs={{1,0},{2,1},{3,2},{4,3},{5,4},{6,5},{7,6},{8,7},{9,8},{10,9},{11,1... | collective-permute-start | bytes 656 | tf_op jit(solution)/shard_map/ppermute | solution.py:28
  197.4 6.5 %collective-permute-start.30 = (f32[1,1,7,25]{3,0,2,1:T(1,128)S(1)}, f32[1,1,7,25]{3,0,2,1:T(1,128)S(1)}, u32[]{:S(2)}, u32[]{:S(2)}) collective-permute-start(f32[1,1,7,25]{3,0,2,1:T(1,128)S(1)} %get-tuple-element.527), channel_id=1, source_target_pairs={{0,128},{128,256},{256,384},{384,512},{512,640},{640,768},{768,896... | collective-permute-start | bytes 2108 | tf_op jit(solution)/shard_map/ppermute | solution.py:26
  200.3 4.4 collective-permute-start.31
  204.8 6.4 %collective-permute-start.32 = (f32[1,6,1,25]{3,0,2,1:T(1,128)S(1)}, f32[1,6,1,25]{3,0,2,1:T(1,128)S(1)}, u32[]{:S(2)}, u32[]{:S(2)}) collective-permute-start(f32[1,6,1,25]{3,0,2,1:T(1,128)S(1)} %get-tuple-element.506), channel_id=1, source_target_pairs={{0,16},{16,32},{32,48},{48,64},{64,80},{80,96},{96,112},{112,0},{1... | collective-permute-start | bytes 1808 | tf_op jit(solution)/shard_map/ppermute | solution.py:26
  206.2 5.1 collective-permute-start.33
  211.5 7.1 %collective-permute-start.34 = (f32[1,6,9,1]{3,0,2,1:T(1,128)S(1)}, f32[1,6,9,1]{3,0,2,1:T(1,128)S(1)}, u32[]{:S(2)}, u32[]{:S(2)}) collective-permute-start(f32[1,6,9,1]{3,0,2,1:T(1,128)S(1)} %get-tuple-element.535), channel_id=1, source_target_pairs={{0,1},{1,2},{2,3},{3,4},{4,5},{5,6},{6,7},{7,8},{8,9},{9,10},{10,1... | collective-permute-start | bytes 656 | tf_op jit(solution)/shard_map/ppermute | solution.py:26
  213.7 5.8 collective-permute-start.35
  222.5 7.0 %collective-permute-start.36 = (f32[1,1,3,9]{3,1,2,0:T(1,128)S(1)}, f32[1,1,3,9]{3,1,2,0:T(1,128)S(1)}, u32[]{:S(2)}, u32[]{:S(2)}) collective-permute-start(f32[1,1,3,9]{3,1,2,0:T(1,128)S(1)} %get-tuple-element.599), channel_id=1, source_target_pairs={{0,128},{128,256},{256,384},{384,512},{512,640},{640,768},{768,896... | collective-permute-start | bytes 332 | tf_op jit(solution)/shard_map/ppermute | solution.py:26
  225.3 4.8 collective-permute-start.37
  230.2 6.1 %collective-permute-start.38 = (f32[1,4,1,9]{3,1,2,0:T(4,128)S(1)}, f32[1,4,1,9]{3,1,2,0:T(4,128)S(1)}, u32[]{:S(2)}, u32[]{:S(2)}) collective-permute-start(f32[1,4,1,9]{3,1,2,0:T(4,128)S(1)} %get-tuple-element.567), channel_id=1, source_target_pairs={{0,16},{16,32},{32,48},{48,64},{64,80},{80,96},{96,112},{112,0},{1... | collective-permute-start | bytes 440 | tf_op jit(solution)/shard_map/ppermute | solution.py:26
  230.2 6.2 %collective-permute-start.39 = (f32[1,4,1,9]{3,1,2,0:T(4,128)S(1)}, f32[1,4,1,9]{3,1,2,0:T(4,128)S(1)}, u32[]{:S(2)}, u32[]{:S(2)}) collective-permute-start(f32[1,4,1,9]{3,1,2,0:T(4,128)S(1)} %get-tuple-element.568), channel_id=1, source_target_pairs={{16,0},{32,16},{48,32},{64,48},{80,64},{96,80},{112,96},{0,112},{1... | collective-permute-start | bytes 440 | tf_op jit(solution)/shard_map/ppermute | solution.py:28
  236.6 7.1 %collective-permute-start.40 = (f32[1,4,5,1]{3,1,2,0:T(4,128)S(1)}, f32[1,4,5,1]{3,1,2,0:T(4,128)S(1)}, u32[]{:S(2)}, u32[]{:S(2)}) collective-permute-start(f32[1,4,5,1]{3,1,2,0:T(4,128)S(1)} %get-tuple-element.563), channel_id=1, source_target_pairs={{0,1},{1,2},{2,3},{3,4},{4,5},{5,6},{6,7},{7,8},{8,9},{9,10},{10,1... | collective-permute-start | bytes 248 | tf_op jit(solution)/shard_map/ppermute | solution.py:26
  239.6 4.8 collective-permute-start.41
  292.9 125.1 %all-gather.10.cloned.1.call-start = ((), (), s32[]{:S(2)}) async-start(), calls=%async_computation.1 | async-start | bytes 8650752 | tf_op jit(solution)/shard_map/all_gather | solution.py:38
  424.4 6.5 %collective-permute-start.42 = (f32[1,1,3,9]{3,1,2,0:T(1,128)S(1)}, f32[1,1,3,9]{3,1,2,0:T(1,128)S(1)}, u32[]{:S(2)}, u32[]{:S(2)}) collective-permute-start(f32[1,1,3,9]{3,1,2,0:T(1,128)S(1)} %get-tuple-element.595), channel_id=1, source_target_pairs={{0,128},{128,256},{256,384},{384,512},{512,640},{640,768},{768,896... | collective-permute-start | bytes 332 | tf_op jit(solution)/shard_map/ppermute | solution.py:26
  426.3 5.3 collective-permute-start.43
  435.7 6.5 %collective-permute-start.46 = (f32[1,4,5,1]{3,1,2,0:T(4,128)S(1)}, f32[1,4,5,1]{3,1,2,0:T(4,128)S(1)}, u32[]{:S(2)}, u32[]{:S(2)}) collective-permute-start(f32[1,4,5,1]{3,1,2,0:T(4,128)S(1)} %get-tuple-element.561), channel_id=1, source_target_pairs={{0,1},{1,2},{2,3},{3,4},{4,5},{5,6},{6,7},{7,8},{8,9},{9,10},{10,1... | collective-permute-start | bytes 248 | tf_op jit(solution)/shard_map/ppermute | solution.py:26
  437.6 5.4 collective-permute-start.47
  446.5 7.1 %collective-permute-start.48 = (f32[1,1,7,25]{3,0,2,1:T(1,128)S(1)}, f32[1,1,7,25]{3,0,2,1:T(1,128)S(1)}, u32[]{:S(2)}, u32[]{:S(2)}) collective-permute-start(f32[1,1,7,25]{3,0,2,1:T(1,128)S(1)} %get-tuple-element.525), channel_id=1, source_target_pairs={{0,128},{128,256},{256,384},{384,512},{512,640},{640,768},{768,896... | collective-permute-start | bytes 2108 | tf_op jit(solution)/shard_map/ppermute | solution.py:26
  448.4 5.8 %collective-permute-start.49 = (f32[1,1,7,25]{3,0,2,1:T(1,128)S(1)}, f32[1,1,7,25]{3,0,2,1:T(1,128)S(1)}, u32[]{:S(2)}, u32[]{:S(2)}) collective-permute-start(f32[1,1,7,25]{3,0,2,1:T(1,128)S(1)} %get-tuple-element.526), channel_id=1, source_target_pairs={{128,0},{256,128},{384,256},{512,384},{640,512},{768,640},{896,768... | collective-permute-start | bytes 2108 | tf_op jit(solution)/shard_map/ppermute | solution.py:28
  454.3 4.6 collective-permute-start.50
  459.6 7.1 %collective-permute-start.52 = (f32[1,6,9,1]{3,0,2,1:T(1,128)S(1)}, f32[1,6,9,1]{3,0,2,1:T(1,128)S(1)}, u32[]{:S(2)}, u32[]{:S(2)}) collective-permute-start(f32[1,6,9,1]{3,0,2,1:T(1,128)S(1)} %get-tuple-element.533), channel_id=1, source_target_pairs={{0,1},{1,2},{2,3},{3,4},{4,5},{5,6},{6,7},{7,8},{8,9},{9,10},{10,1... | collective-permute-start | bytes 656 | tf_op jit(solution)/shard_map/ppermute | solution.py:26
  461.6 6.1 %collective-permute-start.53 = (f32[1,6,9,1]{3,0,2,1:T(1,128)S(1)}, f32[1,6,9,1]{3,0,2,1:T(1,128)S(1)}, u32[]{:S(2)}, u32[]{:S(2)}) collective-permute-start(f32[1,6,9,1]{3,0,2,1:T(1,128)S(1)} %get-tuple-element.534), channel_id=1, source_target_pairs={{1,0},{2,1},{3,2},{4,3},{5,4},{6,5},{7,6},{8,7},{9,8},{10,9},{11,1... | collective-permute-start | bytes 656 | tf_op jit(solution)/shard_map/ppermute | solution.py:28
  471.6 7.1 %collective-permute-start.54 = (f32[1,1,7,25]{3,0,2,1:T(1,128)S(1)}, f32[1,1,7,25]{3,0,2,1:T(1,128)S(1)}, u32[]{:S(2)}, u32[]{:S(2)}) collective-permute-start(f32[1,1,7,25]{3,0,2,1:T(1,128)S(1)} %get-tuple-element.523), channel_id=1, source_target_pairs={{0,128},{128,256},{256,384},{384,512},{512,640},{640,768},{768,896... | collective-permute-start | bytes 2108 | tf_op jit(solution)/shard_map/ppermute | solution.py:26
  475.1 4.6 collective-permute-start.55
  479.8 5.8 collective-permute-start.56
  486.0 7.3 %collective-permute-start.58 = (f32[1,6,9,1]{3,0,2,1:T(1,128)S(1)}, f32[1,6,9,1]{3,0,2,1:T(1,128)S(1)}, u32[]{:S(2)}, u32[]{:S(2)}) collective-permute-start(f32[1,6,9,1]{3,0,2,1:T(1,128)S(1)} %get-tuple-element.531), channel_id=1, source_target_pairs={{0,1},{1,2},{2,3},{3,4},{4,5},{5,6},{6,7},{7,8},{8,9},{9,10},{10,1... | collective-permute-start | bytes 656 | tf_op jit(solution)/shard_map/ppermute | solution.py:26
  489.2 4.9 collective-permute-start.59
  506.4 6.7 %collective-permute-start.60 = (f32[1,1,15,57]{2,1,3,0:T(1,128)S(1)}, f32[1,1,15,57]{2,1,3,0:T(1,128)S(1)}, u32[]{:S(2)}, u32[]{:S(2)}) collective-permute-start(f32[1,1,15,57]{2,1,3,0:T(1,128)S(1)} %get-tuple-element.407), channel_id=1, source_target_pairs={{0,128},{128,256},{256,384},{384,512},{512,640},{640,768},{768,896... | collective-permute-start | bytes 10268 | tf_op jit(solution)/shard_map/ppermute | solution.py:26
  510.0 4.6 collective-permute-start.61
  514.7 6.7 %collective-permute-start.62 = (f32[1,10,1,57]{3,0,2,1:T(1,128)S(1)}, f32[1,10,1,57]{3,0,2,1:T(1,128)S(1)}, u32[]{:S(2)}, u32[]{:S(2)}) collective-permute-start(f32[1,10,1,57]{3,0,2,1:T(1,128)S(1)} %get-tuple-element.438), channel_id=1, source_target_pairs={{0,16},{16,32},{32,48},{48,64},{64,80},{80,96},{96,112},{112,0},{1... | collective-permute-start | bytes 6848 | tf_op jit(solution)/shard_map/ppermute | solution.py:26
  516.5 5.1 collective-permute-start.63
  522.0 7.0 %collective-permute-start.64 = (f32[1,10,17,1]{3,0,2,1:T(1,128)S(1)}, f32[1,10,17,1]{3,0,2,1:T(1,128)S(1)}, u32[]{:S(2)}, u32[]{:S(2)}) collective-permute-start(f32[1,10,17,1]{3,0,2,1:T(1,128)S(1)} %get-tuple-element.430), channel_id=1, source_target_pairs={{0,1},{1,2},{2,3},{3,4},{4,5},{5,6},{6,7},{7,8},{8,9},{9,10},{10,1... | collective-permute-start | bytes 2048 | tf_op jit(solution)/shard_map/ppermute | solution.py:26
  525.6 5.2 collective-permute-start.65
  548.0 6.7 %collective-permute-start.66 = (f32[1,1,15,57]{2,1,3,0:T(1,128)S(1)}, f32[1,1,15,57]{2,1,3,0:T(1,128)S(1)}, u32[]{:S(2)}, u32[]{:S(2)}) collective-permute-start(f32[1,1,15,57]{2,1,3,0:T(1,128)S(1)} %get-tuple-element.405), channel_id=1, source_target_pairs={{0,128},{128,256},{256,384},{384,512},{512,640},{640,768},{768,896... | collective-permute-start | bytes 10268 | tf_op jit(solution)/shard_map/ppermute | solution.py:26
  551.1 4.6 collective-permute-start.67
  555.8 7.0 %collective-permute-start.68 = (f32[1,10,1,57]{3,0,2,1:T(1,128)S(1)}, f32[1,10,1,57]{3,0,2,1:T(1,128)S(1)}, u32[]{:S(2)}, u32[]{:S(2)}) collective-permute-start(f32[1,10,1,57]{3,0,2,1:T(1,128)S(1)} %get-tuple-element.436), channel_id=1, source_target_pairs={{0,16},{16,32},{32,48},{48,64},{64,80},{80,96},{96,112},{112,0},{1... | collective-permute-start | bytes 6848 | tf_op jit(solution)/shard_map/ppermute | solution.py:26
  557.0 6.0 %collective-permute-start.69 = (f32[1,10,1,57]{3,0,2,1:T(1,128)S(1)}, f32[1,10,1,57]{3,0,2,1:T(1,128)S(1)}, u32[]{:S(2)}, u32[]{:S(2)}) collective-permute-start(f32[1,10,1,57]{3,0,2,1:T(1,128)S(1)} %get-tuple-element.437), channel_id=1, source_target_pairs={{16,0},{32,16},{48,32},{64,48},{80,64},{96,80},{112,96},{0,112},{1... | collective-permute-start | bytes 6848 | tf_op jit(solution)/shard_map/ppermute | solution.py:28
  563.3 6.6 %collective-permute-start.70 = (f32[1,10,17,1]{3,0,2,1:T(1,128)S(1)}, f32[1,10,17,1]{3,0,2,1:T(1,128)S(1)}, u32[]{:S(2)}, u32[]{:S(2)}) collective-permute-start(f32[1,10,17,1]{3,0,2,1:T(1,128)S(1)} %get-tuple-element.428), channel_id=1, source_target_pairs={{0,1},{1,2},{2,3},{3,4},{4,5},{5,6},{6,7},{7,8},{8,9},{9,10},{10,1... | collective-permute-start | bytes 2048 | tf_op jit(solution)/shard_map/ppermute | solution.py:26
  566.2 5.2 collective-permute-start.71
  (32 other events, 3762.3 us)
Sparse Core Ops, SparseCore 0:
  293.0 56.3 all-gather.7
  352.0 32.9 all-gather.9
where the time goes:
time: 594 us; the launch traced here: 583 us
  starting transfers between devices  233 us (39%)
  blocking collectives  112 us (19%)
  waiting for transfers between devices  97.5 us (16%)
  local copies, waits for them, and re-layouts  65 us (11%)
  other arithmetic  31.8 us (5%)
  matrix products  22.3 us (4%)
  between operations  22 us (4%)
    ppermute x36, starting transfers between devices, with_halo(): lax.ppermute(head, axis, [((i + 1) % count, i) for i in range(count)])  145 us
    ppermute x36, starting transfers between devices, with_halo(): lax.ppermute(tail, axis, [(i, (i + 1) % count) for i in range(count)])  87.1 us
    all_gather x4, blocking collectives, gathered_by_axis(): nearer = lax.all_gather(array, axes[-1], axis=dim, tiled=True)  72.5 us
    all_gather x2, waiting for transfers between devices, gathered_by_axis(): nearer = lax.all_gather(array, axes[-1], axis=dim, tiled=True)  56.5 us
    unnamed x2, blocking collectives  39.4 us
    ppermute x36, waiting for transfers between devices, with_halo(): lax.ppermute(head, axis, [((i + 1) % count, i) for i in range(count)])  31.9 us
  transfers between devices with their start and end apart: 74, of which 47 were waited for; matrix products, arithmetic and copies ran while one was open for 1% of the time, Pallas kernels for 0%

commit v1 on v0

v1 whole, which is shorter than its diff:
```python
import functools
import math

import jax
import jax.numpy as jnp
import numpy as np
from jax import lax
from jax.experimental import pallas as pl
from jax.experimental.pallas import tpu as pltpu
from jax.sharding import PartitionSpec as P

NF = 8
NM = 4
NC = 2
NE = 16
ROWS = 64
LANES = 128
SLOTS = 4
OPENING = 3
BLOCKS = 11
PLACE = {8: list(range(8)), 4: [0, 1, 2, 7], 2: [0, 7]}
MESH = pl.DeviceIdType.MESH
HIGHEST = lax.Precision.HIGHEST
AREA = [(dx, dy) for dx in (-1, 0, 1) for dy in (-1, 0, 1)]
FLAT = [d for d in AREA if d != (0, 0)]


def legendre_pair(point, degree):
    previous = 1.0
    current = point
    for order in range(1, degree):
        following = ((2 * order + 1) * point * current - order * previous) / (order + 1)
        previous = current
        current = following
    return (current, previous)


def gll_tables(points):
    degree = points - 1
    node_list = []
    for index in range(points):
        guess = -math.cos(math.pi * index / degree)
        for sweep in range(100):
            high_val, low_val = legendre_pair(guess, degree)
            guess = guess - (guess * high_val - low_val) / (points * high_val)
        node_list.append(guess)
    node_list[0] = -1.0
    node_list[degree] = 1.0
    node_pos = np.array(node_list)
    at_nodes = np.array([legendre_pair(value, degree)[0] for value in node_list])
    weights = 2.0 / (degree * (degree + 1) * at_nodes**2)
    derivative = np.zeros((points, points))
    for row_pos in range(points):
        for col_pos in range(points):
            if row_pos != col_pos:
                derivative[row_pos, col_pos] = at_nodes[row_pos] / (
                    at_nodes[col_pos] * (node_pos[row_pos] - node_pos[col_pos])
                )
    derivative[0, 0] = -degree * (degree + 1) / 4.0
    derivative[degree, degree] = degree * (degree + 1) / 4.0
    stiffness = derivative.T @ (weights[:, None] * derivative)
    return (node_pos, weights, stiffness)


def interp_table(fine_pts, coarse_pts):
    fine_nodes = gll_tables(fine_pts)[0]
    coarse_nodes = gll_tables(coarse_pts)[0]
    lagrange = np.ones((fine_pts, coarse_pts))
    for col_pos in range(coarse_pts):
        for other_pos in range(coarse_pts):
            if other_pos != col_pos:
                lagrange[:, col_pos] *= (fine_nodes - coarse_nodes[other_pos]) / (
                    coarse_nodes[col_pos] - coarse_nodes[other_pos]
                )
    return lagrange


def constant_tables():
    parts = {}
    same = np.eye(NE)
    for points in (NF, NM):
        at = PLACE[points]
        _, short_w, short_k = gll_tables(points)
        short_w = short_w.astype(np.float32).astype(np.float64)
        short_k = short_k.astype(np.float32).astype(np.float64)
        w = np.zeros(8)
        w[at] = short_w
        k = np.zeros((8, 8))
        k[np.ix_(at, at)] = short_k
        kd = np.diag(k)
        parts["left%d" % points] = np.concatenate([np.kron(k, np.diag(w)), np.kron(np.diag(w), k)])
        parts["right%d" % points] = np.kron(same, k.T)
        parts["wab%d" % points] = np.repeat(np.kron(w, w)[:, None], LANES, 1)
        lane_w, lane_k = np.tile(w, NE), np.tile(kd, NE)
        parts["dx%d" % points] = np.kron(kd, w)[:, None] * lane_w
        parts["dy%d" % points] = np.kron(w, kd)[:, None] * lane_w
        parts["dz%d" % points] = np.kron(w, w)[:, None] * lane_k
        parts["lane%d" % points] = np.repeat(lane_w[None], 8, 0)
    for fine, coarse, name in ((NF, NM, "f"), (NM, NC, "c")):
        j = np.zeros((8, 8))
        j[np.ix_(PLACE[fine], PLACE[coarse])] = interp_table(fine, coarse)
        parts["down_left_" + name] = np.kron(j, j).T
        parts["down_right_" + name] = np.kron(same, j)
        parts["up_left_" + name] = np.kron(j, j)
        parts["up_right_" + name] = np.kron(same, j.T)
    parts["spread"] = np.kron(same, np.ones((1, 8)))
    ends = ((0, 64), (64, 0), (63, 127), (127, 63))
    pick = np.zeros((32, LANES))
    for index, pair in enumerate(ends):
        for row, lane in enumerate(pair):
            pick[index * 8 + row, lane] = 1.0
    parts["pick"] = pick
    put = np.zeros((8, LANES))
    for row, lane in enumerate((0, 64, 63, 127)):
        put[row, lane] = 1.0
    parts["put"] = put
    own_low, own_top = np.zeros((24, LANES)), np.zeros((24, LANES))
    for z in range(8):
        own_low[z, z * 8] = 1.0
        own_low[8 + z, 64 + z * 8] = 1.0
        own_top[16 + z, 64 + z * 8] = 1.0
    parts["own_low"], parts["own_top"] = own_low, own_top
    start, rows, where = 0, [], {}
    for name, part in parts.items():
        where[name] = (start, part.shape[0], part.shape[1])
        start += part.shape[0]
        rows.append(np.pad(part, ((0, 0), (0, LANES - part.shape[1]))))
    return np.concatenate(rows).astype(np.float32), where


def dot(a, b):
    return jnp.dot(a, b, precision=HIGHEST, preferred_element_type=jnp.float32)


def dot_nt(a, b):
    return lax.dot_general(
        a, b, (((1,), (1,)), ((), ())), precision=HIGHEST, preferred_element_type=jnp.float32
    )


def dot_tn(a, b):
    return lax.dot_general(
        a, b, (((0,), (0,)), ((), ())), precision=HIGHEST, preferred_element_type=jnp.float32
    )


def kernel(
    sizes, where, src_ref, geo_ref, eig_ref, rows_ref, ids_ref, tab_ref, out_ref,
    work, ysend, zsend, xyrecv, zrecv, zin, idsend, idrecv, csend, crecv, colsend, rsrecv,
    zpsend, zprecv, agsend, agrecv, backsend, backrecv,
    xy_sems, z_sems, id_sems, c_sems, rs_sems, zp_sems, ag_sems, back_sems,
):
    n_x, n_y, n_z = sizes
    me_x, me_y, me_z = lax.axis_index("gx"), lax.axis_index("gy"), lax.axis_index("gz")
    bx, by, bz = n_x // 2, n_y // 4, n_z // 2
    my_place = (me_x % 2) * 8 + (me_y % 4) * 2 + me_z % 2
    my_block = (me_x // 2) * by + me_y // 4

    def table(name):
        start, count, width = where[name]
        return tab_ref[pl.ds(start, count), pl.ds(0, width)]

    def near(dx, dy, dz):
        return ((me_x + dx + n_x) % n_x, (me_y + dy + n_y) % n_y, (me_z + dz + n_z) % n_z)

    def mate(ux, uy, uz):
        px, py, pz = (me_x % 2 + ux) % 2, (me_y % 4 + uy) % 4, (me_z % 2 + uz) % 2
        who = ((me_x // 2) * 2 + px, (me_y // 4) * 4 + py, (me_z // 2) * 2 + pz)
        return who, px * 8 + py * 2 + pz

    def across(tx, ty):
        qx, qy = (me_x // 2 + tx) % bx, (me_y // 4 + ty) % by
        return (qx * 2 + me_x % 2, qy * 4 + me_y % 4, me_z), qx * by + qy

    def along(tz):
        return (me_x, me_y, ((me_z // 2 + tz) % bz) * 2 + me_z % 2)

    mates = [mate(i // 8, i // 2 % 4, i % 2) for i in range(1, 16)]
    crosses = [across(i // by, i % by) for i in range(1, bx * by)]
    lines = [along(i) for i in range(1, bz)]

    barrier = pltpu.get_barrier_semaphore()
    peers = [near(dx, dy, dz) for dx, dy in AREA for dz in (-1, 0, 1) if (dx, dy, dz) != (0, 0, 0)]
    peers += [who for who, _ in mates] + [who for who, _ in crosses] + lines
    for who in peers:
        pl.semaphore_signal(barrier, inc=1, device_id=who, device_id_type=MESH)

    def send(src, dst, sems, who):
        pltpu.make_async_remote_copy(
            src_ref=src, dst_ref=dst, send_sem=sems.at[0], recv_sem=sems.at[1],
            device_id=who, device_id_type=MESH,
        ).start()

    def await_all(ref, sems):
        every = pltpu.make_async_remote_copy(
            src_ref=ref, dst_ref=ref, send_sem=sems.at[0], recv_sem=sems.at[1],
            device_id=near(1, 0, 0), device_id_type=MESH,
        )
        every.wait_recv()
        every.wait_send()

    lane = lax.broadcasted_iota(jnp.int32, (8, LANES), 1)
    row = lax.broadcasted_iota(jnp.int32, (8, LANES), 0)
    low_half = lane < 64
    row64 = lax.broadcasted_iota(jnp.int32, (ROWS, LANES), 0)
    lane64 = lax.broadcasted_iota(jnp.int32, (ROWS, LANES), 1)
    node, elem = lane64 % 8, lane64 // 8 % 8
    join_up = (node == 7) & (elem < 7)
    join_down = (node == 0) & (elem > 0)
    edge_y = ((row64 % 8 == 0) & (lane64 < 64)) | ((row64 % 8 == 7) & (lane64 >= 64))
    has_low = (me_y > 0).astype(jnp.float32)
    has_high = (me_y < n_y - 1).astype(jnp.float32)
    at_top = (me_y == n_y - 1).astype(jnp.float32)

    def roll(value, shift, axis):
        return pltpu.roll(value, shift % value.shape[axis], axis)

    def sum_pack(slot, value):
        field = work.at[slot]
        value = (
            value
            + jnp.where(join_up, roll(value, -1, 1), 0.0)
            + jnp.where(join_down, roll(value, 1, 1), 0.0)
        )
        field[pl.ds(0, ROWS), :] = value
        low = field[pl.ds(0, 8, stride=8), :]
        high = field[pl.ds(7, 8, stride=8), :]
        new_low = low + jnp.where(low_half, 0.0, roll(high, 64, 1))
        new_high = high + jnp.where(low_half, roll(low, 64, 1), 0.0)
        field[pl.ds(0, 8, stride=8), :] = new_low
        field[pl.ds(7, 8, stride=8), :] = new_high
        ysend[slot] = jnp.where(low_half, new_low, new_high)
        ends = dot_nt(table("pick"), field[...])
        for index, (dx, dy) in enumerate(AREA):
            keep = low_half
            if dx:
                keep = keep & (lane // 8 == (0 if dx > 0 else 7))
            if dy:
                keep = keep & (lane % 8 == (0 if dy > 0 else 7)) & (row == (0 if dy > 0 else 1))
            for side in (0, 1):
                variant = 2 * side + (1 if dy else 0)
                tile = ends[variant * 8 : variant * 8 + 8]
                moved = jnp.where(keep, roll(tile, -56 * dx - 7 * dy, 1), 0.0)
                zsend[slot, index * 2 + side] = moved[0:2]

    def sum_send(slot):
        for dx, dy in FLAT:
            there = FLAT.index((-dx, -dy))
            if dy:
                src = ysend.at[slot]
            else:
                src = work.at[slot, pl.ds(56 if dx > 0 else 0, 8), :]
            send(src, xyrecv.at[slot, there], xy_sems.at[slot], near(dx, dy, 0))
        for index, (dx, dy) in enumerate(AREA):
            there = AREA.index((-dx, -dy))
            for side, dz in ((0, -1), (1, 1)):
                send(
                    zsend.at[slot, index * 2 + side],
                    zrecv.at[slot, there * 2 + side],
                    z_sems.at[slot],
                    near(dx, dy, dz),
                )

    def sum_finish(slot):
        await_all(xyrecv.at[slot], xy_sems.at[slot])
        tiles = {d: xyrecv[slot, i] for i, d in enumerate(FLAT)}

        def edge(dy):
            return (
                tiles[(0, dy)]
                + jnp.where(row == 7, roll(tiles[(1, dy)], 7, 0), 0.0)
                + jnp.where(row == 0, roll(tiles[(-1, dy)], 1, 0), 0.0)
            )

        from_y = roll(jnp.where(low_half, edge(1) * has_high, edge(-1) * has_low), 64, 1)
        value = work[slot, pl.ds(0, ROWS), :]
        spread = jnp.broadcast_to(from_y[:, None, :], (8, 8, LANES)).reshape(ROWS, LANES)
        value = value + jnp.where(edge_y, spread, 0.0)
        value = value + jnp.concatenate(
            [tiles[(-1, 0)], jnp.zeros((48, LANES), jnp.float32), tiles[(1, 0)]], axis=0
        )
        await_all(zrecv.at[slot], z_sems.at[slot])
        for side in (0, 1):
            parts = []
            for dy in (-1, 0, 1):
                part = sum(zrecv[slot, AREA.index((dx, dy)) * 2 + side] for dx in (-1, 0, 1))
                parts.append(part if dy == 0 else part * (has_low if dy < 0 else has_high))
            target = 2 * (1 - side)
            zin[pl.ds(target, 2), :] = parts[0] + parts[1] + parts[2]
        return value + dot_tn(zin[...], table("put"))[0:ROWS]

    turn = [OPENING]

    def direct_sum(value):
        slot = turn[0] % SLOTS
        turn[0] += 1
        sum_pack(slot, value)
        sum_send(slot)
        return sum_finish(slot)

    for slot in range(SLOTS):
        work[slot, pl.ds(ROWS, ROWS), :] = jnp.zeros((ROWS, LANES), jnp.float32)
    zin[...] = jnp.zeros_like(zin)
    csend[...] = jnp.zeros_like(csend)

    geo = dot(geo_ref[:, 0, :], table("spread")[0:8]) + dot(geo_ref[:, 1, :], table("spread")[8:16])
    geo = [geo[i : i + 1] for i in range(3)]

    spread16 = dot_tn(src_ref[...], table("spread"))
    deep_row = lax.broadcasted_iota(jnp.int32, (NE * 32, LANES), 0)
    deep_lane = lax.broadcasted_iota(jnp.int32, (NE * 32, LANES), 1)
    same_node = deep_row % 8 == deep_lane % 8
    source = jnp.sum(jnp.where(same_node, spread16, 0.0).reshape(ROWS, 8, LANES), axis=1)

    def diagonal(points):
        return sum(g * table("d%s%d" % (axis, points)) for g, axis in zip(geo, "xyz"))

    scaled = {}
    for points in (NF, NM):
        lane_w = table("lane%d" % points)[0:1]
        scaled[points] = (geo[0] * lane_w, geo[1] * lane_w, geo[2] * table("wab%d" % points))

    def local_apply(value, points):
        in_x, in_y, in_z = scaled[points]
        both = dot(table("left%d" % points), value)
        return (
            in_x * both[0:ROWS]
            + in_y * both[ROWS : 2 * ROWS]
            + in_z * dot(value, table("right%d" % points))
        )

    def move(value, way):
        left, right = way.split("-")
        return dot(dot(table(left), value), table(right))

    def cheb_numbers(index):
        lam = jnp.full((1, LANES), eig_ref[index], jnp.float32)
        center = 0.55 * lam
        spread_eig = 0.45 * lam
        ratio = center / spread_eig
        first = 1.0 / ratio
        following = 1.0 / (2.0 * ratio - first)
        return 1.0 / center, first * following, 2.0 * following / spread_eig

    small_lane = lax.broadcasted_iota(jnp.int32, (2, LANES), 1)
    small_row = lax.broadcasted_iota(jnp.int32, (2, LANES), 0)
    spot = small_row * LANES + small_lane - my_place * 16
    own_ids = jnp.zeros((2, LANES), jnp.float32)
    for k in range(BLOCKS):
        number = jnp.full((2, LANES), ids_ref[k], jnp.int32).astype(jnp.float32) + 1.0
        own_ids = jnp.where(spot == k, number, own_ids)
    idsend[...] = own_ids

    sum_pack(0, source)
    sum_pack(1, diagonal(NF))
    sum_pack(2, diagonal(NM))
    pl.semaphore_wait(barrier, len(peers))
    for slot in range(OPENING):
        sum_send(slot)
    for i, (who, _) in enumerate(mates):
        send(idsend, idrecv.at[i], id_sems, who)
    fine_res = sum_finish(0)
    fine_inv = 1.0 / sum_finish(1)
    mid_diag = sum_finish(2)
    mid_inv = jnp.where(mid_diag > 0.0, 1.0 / jnp.where(mid_diag > 0.0, mid_diag, 1.0), 0.0)

    def chebyshev(residual, initial, numbers, points, inverse):
        by_center, first, second = numbers
        if initial is None:
            current = residual
        else:
            current = residual - direct_sum(local_apply(initial, points))
        step_one = inverse * current * by_center
        iterate = step_one if initial is None else initial + step_one
        left = residual - direct_sum(local_apply(iterate, points))
        return iterate + (first * step_one + second * (inverse * left))

    fine_numbers, mid_numbers = cheb_numbers(0), cheb_numbers(1)
    fine_x = chebyshev(fine_res, None, fine_numbers, NF, fine_inv)
    mid_src = move(source - local_apply(fine_x, NF), "down_left_f-down_right_f")
    mid_res = direct_sum(mid_src)
    mid_x = chebyshev(mid_res, None, mid_numbers, NM, mid_inv)
    low_res = direct_sum(move(mid_src - local_apply(mid_x, NM), "down_left_c-down_right_c"))

    own_low = table("own_low")
    own_top = table("own_top") * at_top
    owned = jnp.sum(own_low * low_res[0:1] + own_top * low_res[7:8], axis=1, keepdims=True)
    owned = jnp.broadcast_to(owned, (24, LANES))
    contrib = jnp.zeros((BLOCKS, LANES), jnp.float32)
    for r in range(24):
        contrib = contrib + owned[r : r + 1] * rows_ref[r]
    csend[pl.ds(0, BLOCKS), :] = contrib
    for who, _ in mates:
        send(csend, crecv.at[my_place], c_sems, who)
    crecv[my_place] = csend[...]

    await_all(idrecv, id_sems)
    all_ids = own_ids
    for i in range(15):
        all_ids = all_ids + idrecv[i]
    wanted = (
        lax.broadcasted_iota(jnp.int32, (LANES, LANES), 0) + my_place * LANES + 1
    ).astype(jnp.float32)
    match_a = (all_ids[0:1] == wanted).astype(jnp.float32)
    match_b = (all_ids[1:2] == wanted).astype(jnp.float32)

    await_all(crecv.at[pl.ds(0, 15)], c_sems)
    part = dot(match_a, crecv[pl.ds(0, 8)].reshape(LANES, LANES)) + dot(
        match_b, crecv[pl.ds(8, 8)].reshape(LANES, LANES)
    )
    peers_xy = bx * by
    height = LANES // peers_xy
    colsend[...] = part.reshape(peers_xy, height, LANES)
    for i, (who, block) in enumerate(crosses):
        send(colsend.at[block], rsrecv.at[i], rs_sems, who)
    piece = colsend[my_block]
    await_all(rsrecv, rs_sems)
    for i in range(peers_xy - 1):
        piece = piece + rsrecv[i]
    zpsend[...] = piece
    for i, who in enumerate(lines):
        send(zpsend, zprecv.at[i], zp_sems, who)
    await_all(zprecv, zp_sems)
    for i in range(bz - 1):
        piece = piece + zprecv[i]
    agsend[...] = piece
    for who, _ in crosses:
        send(agsend, agrecv.at[my_block], ag_sems, who)
    agrecv[my_block] = piece
    await_all(agrecv.at[pl.ds(0, peers_xy - 1)], ag_sems)
    slice_sum = agrecv[...].reshape(LANES, LANES)
    backsend[pl.ds(0, 8)] = dot_tn(match_a, slice_sum).reshape(8, 16, LANES)
    backsend[pl.ds(8, 8)] = dot_tn(match_b, slice_sum).reshape(8, 16, LANES)
    for i, (who, place) in enumerate(mates):
        send(backsend.at[place], backrecv.at[i], back_sems, who)
    picked = backsend[my_place]
    await_all(backrecv, back_sems)
    for i in range(15):
        picked = picked + backrecv[i]

    solved = jnp.sum(rows_ref[...] * picked[None, 0:BLOCKS], axis=1)
    solved = jnp.sum(solved, axis=1, keepdims=True)
    at_low = jnp.sum(own_low * solved, axis=0, keepdims=True)
    at_high = jnp.sum(own_top * solved, axis=0, keepdims=True)
    low_u = direct_sum(
        jnp.where(row64 == 0, at_low, 0.0) + jnp.where(row64 == 7, at_high, 0.0)
    )
    mid_x = chebyshev(mid_res, mid_x + move(low_u, "up_left_c-up_right_c"), mid_numbers, NM, mid_inv)
    fine_x = chebyshev(
        fine_res, fine_x + move(mid_x, "up_left_f-up_right_f"), fine_numbers, NF, fine_inv
    )
    deep = jnp.broadcast_to(fine_x[:, None, :], (ROWS, 8, LANES)).reshape(ROWS * 8, LANES)
    out_ref[...] = dot_nt(table("spread"), jnp.where(same_node, deep, 0.0))


def solution(mesh):
    sizes = (mesh.shape["gx"], mesh.shape["gy"], mesh.shape["gz"])
    values, where = constant_tables()
    peers_xy = (sizes[0] // 2) * (sizes[1] // 4)
    height = LANES // peers_xy
    depth = sizes[2] // 2
    f32 = jnp.float32

    def on_device(residual_in, geometry, eig_top, coarse_rows, block_ids):
        vmem = pl.BlockSpec(memory_space=pltpu.VMEM)
        smem = pl.BlockSpec(memory_space=pltpu.SMEM)
        pair = pltpu.SemaphoreType.DMA((2,))
        out = pl.pallas_call(
            functools.partial(kernel, sizes, where),
            out_shape=jax.ShapeDtypeStruct((NE, NF**3), f32),
            in_specs=[vmem, vmem, smem, vmem, smem, vmem],
            out_specs=vmem,
            scratch_shapes=[
                pltpu.VMEM((SLOTS, 2 * ROWS, LANES), f32),
                pltpu.VMEM((SLOTS, 8, LANES), f32),
                pltpu.VMEM((SLOTS, 18, 2, LANES), f32),
                pltpu.VMEM((SLOTS, 8, 8, LANES), f32),
                pltpu.VMEM((SLOTS, 18, 2, LANES), f32),
                pltpu.VMEM((8, LANES), f32),
                pltpu.VMEM((2, LANES), f32),
                pltpu.VMEM((15, 2, LANES), f32),
                pltpu.VMEM((16, LANES), f32),
                pltpu.VMEM((16, 16, LANES), f32),
                pltpu.VMEM((peers_xy, height, LANES), f32),
                pltpu.VMEM((peers_xy - 1, height, LANES), f32),
                pltpu.VMEM((height, LANES), f32),
                pltpu.VMEM((depth - 1, height, LANES), f32),
                pltpu.VMEM((height, LANES), f32),
                pltpu.VMEM((peers_xy, height, LANES), f32),
                pltpu.VMEM((16, 16, LANES), f32),
                pltpu.VMEM((15, 16, LANES), f32),
                pltpu.SemaphoreType.DMA((SLOTS, 2)),
                pltpu.SemaphoreType.DMA((SLOTS, 2)),
                pair, pair, pair, pair, pair, pair,
            ],
            compiler_params=pltpu.CompilerParams(
                collective_id=0, has_side_effects=True, vmem_limit_bytes=32 * 2**20
            ),
        )(
            residual_in.reshape(NE, NF**3),
            geometry.reshape(3, 2, 8),
            eig_top,
            coarse_rows.reshape(24, BLOCKS, LANES),
            block_ids.reshape(BLOCKS),
            jnp.asarray(values),
        )
        return out.reshape(residual_in.shape)

    grid = P("gx", "gy", "gz", None)
    return jax.shard_map(
        on_device,
        mesh=mesh,
        in_specs=(grid, P(None, "gx", "gy", "gz"), P(), P("gx", "gy", "gz", None, None), grid),
        out_specs=grid,
        check_vma=False,
    )
```

time: 594 us -> 119 us (0.20); the launches traced: 583 us -> 119 us
  starting transfers between devices: 233 us -> 0 us
  Pallas kernels: 0 us -> 115 us
  blocking collectives: 112 us -> 0 us
  waiting for transfers between devices: 97.5 us -> 0 us
  local copies, waits for them, and re-layouts: 65 us -> 3.4 us
  other arithmetic: 31.8 us -> 0 us
  matrix products: 22.3 us -> 0 us
  between operations: 22 us -> 0.05 us
    ppermute x72 -> x0, starting transfers between devices: 233 us -> none  [the longest x36 145 us: with_halo(): lax.ppermute(head, axis, [((i + 1) % count, i) for i in range(count)])]
    pallas_call x0 -> x1, Pallas kernels: none -> 115 us  [on_device(): pl.pallas_call(functools.partial(kernel, sizes, where), out_shape=jax.Sha...]
    all_gather x4 -> x0, blocking collectives: 72.5 us -> none  [gathered_by_axis(): nearer = lax.all_gather(array, axes[-1], axis=dim, tiled=True)]
    all_gather x2 -> x0, waiting for transfers between devices: 56.5 us -> none  [gathered_by_axis(): nearer = lax.all_gather(array, axes[-1], axis=dim, tiled=True)]
    ppermute x72 -> x0, waiting for transfers between devices: 41.1 us -> none  [the longest x36 31.9 us: with_halo(): lax.ppermute(head, axis, [((i + 1) % count, i) for i in range(count)])]
    unnamed x2 -> x0, blocking collectives: 39.4 us -> none
    dot_general x39 -> x0, matrix products: 22.3 us -> none  [the longest x1 4.65 us: coarse_solve(): jnp.dot(matches, gathered_by_axis(contrib, ('gy_1', 'gy_0', 'gz', 'gx'),...]
    slice x149 -> x0, local copies, waits for them, and re-layouts: 20.4 us -> none  [the longest x24 7.25 us: fold_axis(): lax.slice_in_dim(point_grid, 0, degree, axis=elem_axis + 1)]
  transfers between devices with their start and end apart: 74 -> 0, of which waited for: 47 -> 0; matrix products, arithmetic and copies ran while one was open for 1% -> 0% of each run, Pallas kernels for 0% -> 0%
where the time goes in v1:
time: 119 us
  Pallas kernels  115 us (97%)
  local copies, waits for them, and re-layouts  3.4 us (3%)
    pallas_call x1, Pallas kernels, on_device(): pl.pallas_call(functools.partial(kernel, sizes, where), out_shape=jax.Sha...  115 us
    unnamed x12, local copies, waits for them, and re-layouts  3.4 us

profile of v1, /device:TPU:1, one launch (start us, length us, event | category | flops | bytes accessed | tf_op | source)
XLA Modules:
  0.0 118.7 jit_solution(6112076647281128133)
XLA Ops:
  0.0 0.0 copy-start.1
  0.0 0.0 copy-start.2
  0.0 0.9 copy.7
  0.9 0.0 copy-start.3
  1.0 0.0 copy-start.4
  1.0 0.0 copy-done.1
  1.0 0.0 copy-done.2
  1.0 0.6 copy-done.3
  1.6 0.0 copy-done.4
  1.6 0.0 copy-start
  1.6 1.2 %copy-done = f32[1912,128]{1,0:T(8,128)S(1)} copy-done((f32[1912,128]{1,0:T(8,128)S(1)}, f32[1912,128]{1,0:T(8,128)}, u32[]{:S(2)}) %copy-start) | copy-done | bytes 978968
  2.8 115.2 %shard_map.64 = f32[16,512]{1,0:T(8,128)S(1)} custom-call(f32[16,512]{1,0:T(8,128)S(1)} %bitcast.7, f32[3,2,8]{2,1,0:T(2,128)S(1)} %bitcast.8, f32[2]{0:T(128)S(1)} %copy-done.3, f32[24,11,128]{2,1,0:T(8,128)S(1)} %bitcast.5, s32[11]{0:T(128)S(1)} %bitcast.9, f32[1912,128]{1,0:T(8,128)S(1)} %copy-done), custom_call_target="tpu_custom_call" | custom-call | tf_op jit(solution)/shard_map/pallas_call | solution.py:468
  118.1 0.6 copy.9
Async XLA Ops:
  0.0 1.0 copy-start.1
  0.0 1.0 copy-start.2
  0.9 0.7 copy-start.3
  1.0 0.7 copy-start.4
  1.6 1.2 %copy-start = (f32[1912,128]{1,0:T(8,128)S(1)}, f32[1912,128]{1,0:T(8,128)}, u32[]{:S(2)}) copy-start(f32[1912,128]{1,0:T(8,128)} %constant.2.clone.tab_ref) | copy-start | bytes 2936836

commit v2 on v1

--- a/solution.py
+++ b/solution.py
@@ -132,6 +132,20 @@
     return jnp.dot(a, b, precision=HIGHEST, preferred_element_type=jnp.float32)
 
 
+def split(value):
+    high = value.astype(jnp.bfloat16)
+    return high, (value - high.astype(jnp.float32)).astype(jnp.bfloat16)
+
+
+def dot3(a, b):
+    (a_high, a_low), (b_high, b_low) = split(a), split(b)
+
+    def one(left, right):
+        return jnp.dot(left, right, preferred_element_type=jnp.float32)
+
+    return one(a_high, b_high) + (one(a_high, b_low) + one(a_low, b_high))
+
+
 def dot_nt(a, b):
     return lax.dot_general(
         a, b, (((1,), (1,)), ((), ())), precision=HIGHEST, preferred_element_type=jnp.float32
@@ -145,12 +159,19 @@
 
 
 def kernel(
-    sizes, where, src_ref, geo_ref, eig_ref, rows_ref, ids_ref, tab_ref, out_ref,
-    work, ysend, zsend, xyrecv, zrecv, zin, idsend, idrecv, csend, crecv, colsend, rsrecv,
+    sizes, where, src_far, geo_ref, eig_ref, rows_far, ids_ref, tab_far, out_ref,
+    src_ref, rows_ref, tab_ref, near_sems, work, ysend, zsend, xyrecv, zrecv, zin, idsend, idrecv, csend, crecv, colsend, rsrecv,
     zpsend, zprecv, agsend, agrecv, backsend, backrecv,
     xy_sems, z_sems, id_sems, c_sems, rs_sems, zp_sems, ag_sems, back_sems,
 ):
     n_x, n_y, n_z = sizes
+    fetch_tab = pltpu.make_async_copy(tab_far, tab_ref, near_sems.at[0])
+    fetch_rows = pltpu.make_async_copy(rows_far, rows_ref, near_sems.at[1])
+    fetch_src = pltpu.make_async_copy(src_far, src_ref, near_sems.at[2])
+    fetch_src.start()
+    fetch_tab.start()
+    fetch_rows.start()
+    crecv[...] = jnp.zeros_like(crecv)
     me_x, me_y, me_z = lax.axis_index("gx"), lax.axis_index("gy"), lax.axis_index("gz")
     bx, by, bz = n_x // 2, n_y // 4, n_z // 2
     my_place = (me_x % 2) * 8 + (me_y % 4) * 2 + me_z % 2
@@ -243,26 +264,28 @@
                 moved = jnp.where(keep, roll(tile, -56 * dx - 7 * dy, 1), 0.0)
                 zsend[slot, index * 2 + side] = moved[0:2]
 
-    def sum_send(slot):
-        for dx, dy in FLAT:
-            there = FLAT.index((-dx, -dy))
-            if dy:
-                src = ysend.at[slot]
+    def sum_send(slot, fields=1):
+        span = pl.ds(slot, fields)
+        order = [(dx, dy, dz) for dx, dy in AREA for dz in (-1, 0, 1) if (dx, dy, dz) != (0, 0, 0)]
+        for dx, dy, dz in sorted(order, key=lambda d: -sum(map(abs, d))):
+            if dz:
+                side = 0 if dz < 0 else 1
+                src = zsend.at[span, AREA.index((dx, dy)) * 2 + side]
+                dst = zrecv.at[span, AREA.index((-dx, -dy)) * 2 + side]
+                send(src, dst, z_sems.at[slot], near(dx, dy, dz))
             else:
-                src = work.at[slot, pl.ds(56 if dx > 0 else 0, 8), :]
-            send(src, xyrecv.at[slot, there], xy_sems.at[slot], near(dx, dy, 0))
-        for index, (dx, dy) in enumerate(AREA):
-            there = AREA.index((-dx, -dy))
-            for side, dz in ((0, -1), (1, 1)):
-                send(
-                    zsend.at[slot, index * 2 + side],
-                    zrecv.at[slot, there * 2 + side],
-                    z_sems.at[slot],
-                    near(dx, dy, dz),
-                )
+                if dy:
+                    src = ysend.at[span]
+                else:
+                    src = work.at[span, pl.ds(56 if dx > 0 else 0, 8), :]
+                dst = xyrecv.at[span, FLAT.index((-dx, -dy))]
+                send(src, dst, xy_sems.at[slot], near(dx, dy, dz))
+
+    def sum_await(slot, fields=1):
+        await_all(xyrecv.at[pl.ds(slot, fields)], xy_sems.at[slot])
+        await_all(zrecv.at[pl.ds(slot, fields)], z_sems.at[slot])
 
     def sum_finish(slot):
-        await_all(xyrecv.at[slot], xy_sems.at[slot])
         tiles = {d: xyrecv[slot, i] for i, d in enumerate(FLAT)}
 
         def edge(dy):
@@ -279,7 +302,6 @@
         value = value + jnp.concatenate(
             [tiles[(-1, 0)], jnp.zeros((48, LANES), jnp.float32), tiles[(1, 0)]], axis=0
         )
-        await_all(zrecv.at[slot], z_sems.at[slot])
         for side in (0, 1):
             parts = []
             for dy in (-1, 0, 1):
@@ -296,12 +318,14 @@
         turn[0] += 1
         sum_pack(slot, value)
         sum_send(slot)
+        sum_await(slot)
         return sum_finish(slot)
 
+    fetch_src.wait()
+    fetch_tab.wait()
     for slot in range(SLOTS):
         work[slot, pl.ds(ROWS, ROWS), :] = jnp.zeros((ROWS, LANES), jnp.float32)
     zin[...] = jnp.zeros_like(zin)
-    csend[...] = jnp.zeros_like(csend)
 
     geo = dot(geo_ref[:, 0, :], table("spread")[0:8]) + dot(geo_ref[:, 1, :], table("spread")[8:16])
     geo = [geo[i : i + 1] for i in range(3)]
@@ -322,16 +346,16 @@
 
     def local_apply(value, points):
         in_x, in_y, in_z = scaled[points]
-        both = dot(table("left%d" % points), value)
+        both = dot3(table("left%d" % points), value)
         return (
             in_x * both[0:ROWS]
             + in_y * both[ROWS : 2 * ROWS]
-            + in_z * dot(value, table("right%d" % points))
+            + in_z * dot3(value, table("right%d" % points))
         )
 
     def move(value, way):
         left, right = way.split("-")
-        return dot(dot(table(left), value), table(right))
+        return dot3(dot3(table(left), value), table(right))
 
     def cheb_numbers(index):
         lam = jnp.full((1, LANES), eig_ref[index], jnp.float32)
@@ -355,10 +379,10 @@
     sum_pack(1, diagonal(NF))
     sum_pack(2, diagonal(NM))
     pl.semaphore_wait(barrier, len(peers))
-    for slot in range(OPENING):
-        sum_send(slot)
+    sum_send(0, OPENING)
     for i, (who, _) in enumerate(mates):
         send(idsend, idrecv.at[i], id_sems, who)
+    sum_await(0, OPENING)
     fine_res = sum_finish(0)
     fine_inv = 1.0 / sum_finish(1)
     mid_diag = sum_finish(2)
@@ -385,14 +409,16 @@
     own_low = table("own_low")
     own_top = table("own_top") * at_top
     owned = jnp.sum(own_low * low_res[0:1] + own_top * low_res[7:8], axis=1, keepdims=True)
-    owned = jnp.broadcast_to(owned, (24, LANES))
-    contrib = jnp.zeros((BLOCKS, LANES), jnp.float32)
-    for r in range(24):
-        contrib = contrib + owned[r : r + 1] * rows_ref[r]
-    csend[pl.ds(0, BLOCKS), :] = contrib
+    owned = jnp.broadcast_to(owned, (24, LANES)).reshape(3, 8, LANES)
+    fetch_rows.wait()
+    contrib = (
+        owned[0:1] * rows_ref[0] + owned[1:2] * rows_ref[1] + owned[2:3] * rows_ref[2]
+    )
+    contrib = jnp.sum(contrib, axis=1)
+    csend[...] = contrib
     for who, _ in mates:
-        send(csend, crecv.at[my_place], c_sems, who)
-    crecv[my_place] = csend[...]
+        send(csend, crecv.at[my_place, pl.ds(0, BLOCKS)], c_sems, who)
+    crecv[my_place, pl.ds(0, BLOCKS)] = contrib
 
     await_all(idrecv, id_sems)
     all_ids = own_ids
@@ -404,7 +430,7 @@
     match_a = (all_ids[0:1] == wanted).astype(jnp.float32)
     match_b = (all_ids[1:2] == wanted).astype(jnp.float32)
 
-    await_all(crecv.at[pl.ds(0, 15)], c_sems)
+    await_all(crecv.at[pl.ds(0, 15), pl.ds(0, BLOCKS)], c_sems)
     part = dot(match_a, crecv[pl.ds(0, 8)].reshape(LANES, LANES)) + dot(
         match_b, crecv[pl.ds(8, 8)].reshape(LANES, LANES)
     )
@@ -432,13 +458,15 @@
     backsend[pl.ds(0, 8)] = dot_tn(match_a, slice_sum).reshape(8, 16, LANES)
     backsend[pl.ds(8, 8)] = dot_tn(match_b, slice_sum).reshape(8, 16, LANES)
     for i, (who, place) in enumerate(mates):
-        send(backsend.at[place], backrecv.at[i], back_sems, who)
-    picked = backsend[my_place]
+        send(backsend.at[place, pl.ds(0, BLOCKS)], backrecv.at[i], back_sems, who)
+    picked = backsend[my_place, pl.ds(0, BLOCKS)]
     await_all(backrecv, back_sems)
     for i in range(15):
         picked = picked + backrecv[i]
 
-    solved = jnp.sum(rows_ref[...] * picked[None, 0:BLOCKS], axis=1)
+    solved = jnp.concatenate(
+        [sum(rows_ref[j, k] * picked[k : k + 1] for k in range(BLOCKS)) for j in range(3)], axis=0
+    )
     solved = jnp.sum(solved, axis=1, keepdims=True)
     at_low = jnp.sum(own_low * solved, axis=0, keepdims=True)
     at_high = jnp.sum(own_top * solved, axis=0, keepdims=True)
@@ -464,13 +492,18 @@
     def on_device(residual_in, geometry, eig_top, coarse_rows, block_ids):
         vmem = pl.BlockSpec(memory_space=pltpu.VMEM)
         smem = pl.BlockSpec(memory_space=pltpu.SMEM)
+        far = pl.BlockSpec(memory_space=pltpu.HBM)
         pair = pltpu.SemaphoreType.DMA((2,))
         out = pl.pallas_call(
             functools.partial(kernel, sizes, where),
             out_shape=jax.ShapeDtypeStruct((NE, NF**3), f32),
-            in_specs=[vmem, vmem, smem, vmem, smem, vmem],
+            in_specs=[far, vmem, smem, far, smem, far],
             out_specs=vmem,
             scratch_shapes=[
+                pltpu.VMEM((NE, NF**3), f32),
+                pltpu.VMEM((3, BLOCKS, 8, LANES), f32),
+                pltpu.VMEM(values.shape, f32),
+                pltpu.SemaphoreType.DMA((3,)),
                 pltpu.VMEM((SLOTS, 2 * ROWS, LANES), f32),
                 pltpu.VMEM((SLOTS, 8, LANES), f32),
                 pltpu.VMEM((SLOTS, 18, 2, LANES), f32),
@@ -479,7 +512,7 @@
                 pltpu.VMEM((8, LANES), f32),
                 pltpu.VMEM((2, LANES), f32),
                 pltpu.VMEM((15, 2, LANES), f32),
-                pltpu.VMEM((16, LANES), f32),
+                pltpu.VMEM((BLOCKS, LANES), f32),
                 pltpu.VMEM((16, 16, LANES), f32),
                 pltpu.VMEM((peers_xy, height, LANES), f32),
                 pltpu.VMEM((peers_xy - 1, height, LANES), f32),
@@ -488,19 +521,19 @@
                 pltpu.VMEM((height, LANES), f32),
                 pltpu.VMEM((peers_xy, height, LANES), f32),
                 pltpu.VMEM((16, 16, LANES), f32),
-                pltpu.VMEM((15, 16, LANES), f32),
+                pltpu.VMEM((15, BLOCKS, LANES), f32),
                 pltpu.SemaphoreType.DMA((SLOTS, 2)),
                 pltpu.SemaphoreType.DMA((SLOTS, 2)),
                 pair, pair, pair, pair, pair, pair,
             ],
             compiler_params=pltpu.CompilerParams(
-                collective_id=0, has_side_effects=True, vmem_limit_bytes=32 * 2**20
+                collective_id=0, has_side_effects=True
             ),
         )(
             residual_in.reshape(NE, NF**3),
             geometry.reshape(3, 2, 8),
             eig_top,
-            coarse_rows.reshape(24, BLOCKS, LANES),
+            jnp.swapaxes(coarse_rows.reshape(3, 8, BLOCKS, LANES), 1, 2),
             block_ids.reshape(BLOCKS),
             jnp.asarray(values),
         )

time: 119 us -> 116 us (0.975)
  local copies, waits for them, and re-layouts: 3.4 us -> 1.38 us
    unnamed x12 -> x1, local copies, waits for them, and re-layouts: 3.4 us -> 1.38 us
where the time goes in v2:
time: 116 us
  Pallas kernels  115 us (99%)
  local copies, waits for them, and re-layouts  1.38 us (1%)
    pallas_call x1, Pallas kernels, on_device(): pl.pallas_call(functools.partial(kernel, sizes, where), out_shape=jax.Sha...  115 us

profile of v2, /device:TPU:1, one launch (start us, length us, event | category | flops | bytes accessed | tf_op | source)
XLA Modules:
  0.0 115.9 jit_solution(17000360065072453387)
XLA Ops:
  0.0 114.6 %shard_map.64 = f32[16,512]{1,0:T(8,128)} custom-call(f32[16,512]{1,0:T(8,128)} %bitcast.9, f32[3,2,8]{2,1,0:T(2,128)} %bitcast.10, f32[2]{0:T(128)} %eig_ref.1, f32[3,11,8,128]{3,2,1,0:T(8,128)} %bitcast.7, s32[11]{0:T(128)} %bitcast.11, f32[1912,128]{1,0:T(8,128)} %constant.2.clone.tab_far), custom_call_target="tpu_custom_call" | custom-call | tf_op jit(solution)/shard_map/pallas_call | solution.py:497
  114.6 1.4 %copy.8 = f32[1,2,8,512]{3,2,1,0:T(8,128)} copy(f32[1,2,8,512]{3,2,1,0:T(8,128)} %bitcast.8) | data formatting | bytes 65536

commit v3 on v2

--- a/solution.py
+++ b/solution.py
@@ -527,7 +527,7 @@
                 pair, pair, pair, pair, pair, pair,
             ],
             compiler_params=pltpu.CompilerParams(
-                collective_id=0, has_side_effects=True
+                collective_id=0, has_side_effects=True, vmem_limit_bytes=56500000
             ),
         )(
             residual_in.reshape(NE, NF**3),

time: 116 us -> 115 us (level)
  no operation moved by 1% of the time
where the time goes in v3:
time: 115 us
  Pallas kernels  114 us (99%)
  local copies, waits for them, and re-layouts  1.3 us (1%)
    pallas_call x1, Pallas kernels, on_device(): pl.pallas_call(functools.partial(kernel, sizes, where), out_shape=jax.Sha...  114 us

profile of v3, /device:TPU:1, one launch (start us, length us, event | category | flops | bytes accessed | tf_op | source)
XLA Modules:
  0.0 115.0 jit_solution(6107899921916012315)
XLA Ops:
  0.0 0.0 copy-start
  0.0 0.0 copy-start.1
  0.0 0.0 copy-start.2
  0.0 0.7 copy-done
  0.7 0.0 copy-done.1
  0.7 0.0 copy-done.2
  0.7 113.7 %shard_map.64 = f32[16,512]{1,0:T(8,128)S(1)} custom-call(f32[16,512]{1,0:T(8,128)} %bitcast.11, f32[3,2,8]{2,1,0:T(2,128)S(1)} %bitcast.8, f32[2]{0:T(128)S(1)} %copy-done.1, f32[3,11,8,128]{3,2,1,0:T(8,128)} %bitcast.10, s32[11]{0:T(128)S(1)} %bitcast.9, f32[1912,128]{1,0:T(8,128)} %constant.2.clone.tab_far), custom_call_target="tpu_custom_call" | custom-call | tf_op jit(solution)/shard_map/pallas_call | solution.py:497
  114.4 0.6 copy.8
Async XLA Ops:
  0.0 0.7 copy-start
  0.0 0.7 copy-start.1
  0.0 0.7 copy-start.2
